TPU v7x, 256 devices: a whole 4x4x8 slice. The times are simulated.
256 devices in a mesh: gx: 4 (over y), gy: 8 (over x, core), gz: 8 (over z).
Axes of the slice: x: 4, y: 4, z: 8, core: 2. Of those that a mesh axis runs over, the one named last changes fastest.
Arguments:
- start_block: float32 [64, 3, 8, 64, 1024], P(None, None, 'gx', 'gy', 'gz'), may hold values from -6 to 6
- stiff_field: float32 [8, 64, 1024], P('gx', 'gy', 'gz'), may hold values from 0.5 to 2
- shift_field: float32 [8, 64, 1024], P('gx', 'gy', 'gz'), may hold values from 0.25 to 2
- mass_field: float32 [8, 64, 1024], P('gx', 'gy', 'gz'), may hold values from 0.5 to 2
Outputs:
- modes: float32 [64, 3, 8, 64, 1024], P(None, None, 'gx', 'gy', 'gz')
- ritz: float32 [64, 64], replicated
All inputs are finite; a program needn't handle non-finite values. Where the computation divides by a largest or mean magnitude, that divisor is 1e-20 or more.
Results may differ from a plain program's by a relative error of at most 0.0003.
Values sent between devices are 32-bit elements; how exact they have to be, the bound alone decides.
A program may use at most 128 MiB of HBM per device.

v0:
```python
import functools

import jax
import jax.numpy as jnp
from jax import lax
from jax.experimental import pallas as pl
from jax.experimental.pallas import tpu as pltpu
from jax.sharding import PartitionSpec as P

MESH = pl.DeviceIdType.MESH
F32 = jnp.float32
NV = 64
T = 128
NX, NC, NY = 2, 3, 8
PLANE = NC * NY * T
COLS = NX * PLANE
EDGE = NX * NC * T
X_LO, X_HI = 0, PLANE
Y_LO, Y_HI = 2 * PLANE, 2 * PLANE + EDGE
Z_AT = 2 * PLANE + 2 * EDGE
HALO = Z_AT + T
CH = NY * T
FAR_FIRST = {4: (2, 1, 3), 8: (4, 3, 5, 2, 6, 1, 7)}


def mm(a, b, ca=1, cb=0):
    return lax.dot_general(
        a, b, (((ca,), (cb,)), ((), ())), precision=lax.Precision.HIGHEST, preferred_element_type=F32
    )


def nt(a, b):
    return mm(a, b, 1, 1)


def tn(a, b):
    return mm(a, b, 0, 0)


def eye(n):
    return jnp.where(
        lax.broadcasted_iota(jnp.int32, (n, n), 0) == lax.broadcasted_iota(jnp.int32, (n, n), 1), 1.0, 0.0
    ).astype(F32)


def factor_inverse(a):
    n, p = NV, 8
    m = jnp.concatenate([a, eye(n)], axis=1)

    def full(x):
        return jnp.broadcast_to(x, (8, 2 * n))

    rows = [m[8 * i : 8 * i + 8, :] for i in range(n // 8)]
    sub = lax.broadcasted_iota(jnp.int32, (8, 2 * n), 0)
    pivots = []
    for v in range(n // 8):
        k = v * 8
        col = [{i: full(rows[i][:, k + t : k + t + 1]) for i in range(v, 8)} for t in range(p)]
        blk = [[full(col[u][v][t : t + 1, :]) if u <= t else None for u in range(p)] for t in range(p)]
        row = [full(rows[v][t : t + 1, :]) for t in range(p)]
        fac, piv = [None] * p, [None] * p
        for a_ in range(0, p, 2):
            b_ = a_ + 1
            i0 = 1.0 / blk[a_][a_]
            det = blk[a_][a_] * blk[b_][b_] - blk[b_][a_] * blk[b_][a_]
            i1 = blk[a_][a_] * (1.0 / det)
            low = blk[b_][a_] * i0
            piv[a_] = blk[a_][a_]
            piv[b_] = blk[b_][b_] - low * blk[b_][a_]
            row[b_] = row[b_] - low * row[a_]
            f0 = {i: col[a_][i] * i0 for i in range(v, 8)}
            f1 = {i: (col[b_][i] - col[a_][i] * low) * i1 for i in range(v, 8)}
            fac[a_], fac[b_] = f0, f1
            h0, g1, h1 = {}, {}, {}
            for t in range(b_ + 1, p):
                h0[t] = blk[t][a_] * i0
                g1[t] = blk[t][b_] - h0[t] * blk[b_][a_]
                h1[t] = g1[t] * i1
            for t in range(b_ + 1, p):
                for u in range(b_ + 1, t + 1):
                    blk[t][u] = blk[t][u] - h0[t] * blk[u][a_] - h1[t] * g1[u]
                row[t] = row[t] - h0[t] * row[a_] - h1[t] * row[b_]
                for i in range(v, 8):
                    col[t][i] = col[t][i] - f0[i] * blk[t][a_] - f1[i] * g1[t]
        d = piv[0]
        for t in range(1, p):
            d = jnp.where(sub >= t, piv[t], d)
        pivots.append(d)
        for i in range(v, 8):
            acc = None
            for t in range(p):
                if i == v and t == 7:
                    continue
                f = fac[t][i]
                if i == v:
                    f = jnp.where(sub > t, f, 0.0)
                acc = f * row[t] if acc is None else acc + f * row[t]
            rows[i] = rows[i] - acc
    return jnp.concatenate([r * lax.rsqrt(d) for r, d in zip(rows, pivots)], axis=0)[:, n:]


def filtered(h):
    n = h.shape[0]
    bound = jnp.max(jnp.sum(jnp.abs(h), axis=1, keepdims=True), axis=0, keepdims=True)
    f = eye(n) - h / bound
    f2 = mm(f, f)
    y = mm(f2, f2[:, :NV])
    qt = nt(factor_inverse(tn(y, y)), y)
    th = mm(qt, h)
    return qt, th, nt(th, qt)


def kernel(
    dofs, sizes,
    s, g, e, rho, out, ritz,
    V, KV, H, BR, OB, HB, HS, QF, QX, QH, YP, YK, YR, ZK, ZR, CO,
    P0, P1, P2, A0, A1, A2, B0, B1, B2, C0, C1, C2, D0, D1, D2,
    SM, ar_sem, halo_sem,
):
    me = {a: lax.axis_index(a) for a in ("gx", "gy", "gz")}
    lane = lax.broadcasted_iota(jnp.int32, (8, T), 1)

    def peer(axis, off):
        return lax.rem(me[axis] + off, sizes[axis])

    barrier = pltpu.get_barrier_semaphore()
    zero, one = jnp.zeros((NV, NV), F32), eye(NV)
    for axis in ("gx", "gy", "gz"):
        for off in FAR_FIRST[sizes[axis]]:
            pl.semaphore_signal(barrier, inc=1, device_id={axis: peer(axis, off)}, device_id_type=MESH)

    def remote(src, dst, send, recv, axis, to):
        return pltpu.make_async_remote_copy(
            src_ref=src, dst_ref=dst, send_sem=send, recv_sem=recv, device_id={axis: to}, device_id_type=MESH
        )

    def tile(k):
        return slice(k * T, (k + 1) * T)

    def at(x, c, y):
        return (x * NC + c) * NY + y

    def block(start, n=8):
        return pl.ds(pl.multiple_of(start, 8), n)

    diag = 6.0 * g[...] * g[...] + 1.5 * e[...]
    inv = 1.0 / diag
    CO[0] = inv
    CO[1] = rho[...] * inv
    CO[2] = g[...] * inv

    def load(b, _):
        up, down = jnp.zeros((8, T), F32), jnp.zeros((8, T), F32)
        rows = block(b * 8)
        for x in range(NX):
            for y in range(NY):
                r = x * NY + y
                gr, qr, mr = g[r : r + 1, :], CO[1, r : r + 1, :], rho[r : r + 1, :]
                for c in range(NC):
                    k = at(x, c, y)
                    v = s[pl.ds(b * 384 + (c * NX + x) * NY + y, 8, stride=48), :]
                    h = gr * v
                    V[rows, tile(k)] = v
                    H[rows, tile(k)] = h
                    BR[rows, tile(k)] = mr * v
                    OB[block(NV + b * 8), tile(k)] = qr * v
                    if y == NY - 1:
                        YK[0, rows, tile(x * NC + c)] = h
                    if y == 0:
                        YK[1, rows, tile(x * NC + c)] = h
                    up = jnp.where(lane == 2 * k, pltpu.roll(h, (2 * k + 1) % T, 1), up)
                    down = jnp.where(lane == (2 * k - 1) % T, pltpu.roll(h, (2 * k - 1) % T, 1), down)
        ZK[0, rows, :] = up
        ZK[1, rows, :] = down
        return 0

    lax.fori_loop(0, NV // 8, load, 0)
    up, down = jnp.zeros((8, T), F32), jnp.zeros((8, T), F32)
    for x in range(NX):
        for y in range(NY):
            q = jnp.broadcast_to(CO[1, x * NY + y : x * NY + y + 1, :], (8, T))
            QF[:, tile(x * NY + y)] = q
            for c in range(NC):
                k = at(x, c, y)
                if y == NY - 1:
                    YK[0, NV : NV + 8, tile(x * NC + c)] = q
                if y == 0:
                    YK[1, NV : NV + 8, tile(x * NC + c)] = q
                up = jnp.where(lane == 2 * k, pltpu.roll(q, (2 * k + 1) % T, 1), up)
                down = jnp.where(lane == (2 * k - 1) % T, pltpu.roll(q, (2 * k - 1) % T, 1), down)
    ZK[0, NV : NV + 8, :] = up
    ZK[1, NV : NV + 8, :] = down

    pl.semaphore_wait(barrier, sum(sizes.values()) - 3)

    all_rows = pl.ds(0, NV)

    def exchange(n, faces):
        started, arrived = [], []
        for i, (axis, up_src, down_src, low, high) in enumerate(faces):
            here, size = me[axis], sizes[axis]
            up_copy = remote(
                up_src, low, halo_sem.at[n, 0, 2 * i], halo_sem.at[n, 1, 2 * i], axis, lax.rem(here + 1, size)
            )
            down_copy = remote(
                down_src, high, halo_sem.at[n, 0, 2 * i + 1], halo_sem.at[n, 1, 2 * i + 1],
                axis, lax.rem(here + size - 1, size),
            )
            started += [(here < size - 1, up_copy), (here > 0, down_copy)]
            arrived += [(here > 0, up_copy, low), (here < size - 1, down_copy, high)]

        def start():
            for cond, copy in started:
                pl.when(cond)(copy.start)

        def wait():
            for cond, copy, place in arrived:
                pl.when(cond)(copy.wait_recv)

                @pl.when(jnp.logical_not(cond))
                def _():
                    place[...] = jnp.zeros(place.shape, F32)

        def finish():
            for cond, copy in started:
                pl.when(cond)(copy.wait_send)

        return start, wait, finish

    first = exchange(0, [
        ("gx", H.at[:, PLANE:COLS], H.at[:, 0:PLANE], HS.at[0, :, X_LO : X_LO + PLANE], HS.at[0, :, X_HI : X_HI + PLANE]),
        ("gx", QF.at[:, CH : 2 * CH], QF.at[:, 0:CH], QX.at[0], QX.at[1]),
        ("gy", YK.at[0], YK.at[1], YR.at[0], YR.at[1]),
        ("gz", ZK.at[0], ZK.at[1], ZR.at[0, 0], ZR.at[0, 1]),
    ])

    def later(n):
        top = 2 * NV * (n - 1)
        row = pl.ds(top, NV)
        return exchange(n, [
            ("gz", ZK.at[2 * n, 0:NV], ZK.at[2 * n + 1, 0:NV], ZR.at[n, 0, 0:NV], ZR.at[n, 1, 0:NV]),
            ("gy", YK.at[2 * n, 0:NV], YK.at[2 * n + 1, 0:NV], HB.at[row, Y_LO : Y_LO + EDGE], HB.at[row, Y_HI : Y_HI + EDGE]),
            ("gx", YP.at[n - 1, :, PLANE:COLS], YP.at[n - 1, :, 0:PLANE], HB.at[row, X_LO : X_LO + PLANE], HB.at[row, X_HI : X_HI + PLANE]),
        ])

    def stiffness(n, again):
        row = n * NV

        def body(b, _):
            up, down = jnp.zeros((8, T), F32), jnp.zeros((8, T), F32)
            rows, full = block(b * 8), block(row + b * 8)
            ends = HS[n % 2, rows, Z_AT:HALO]
            for x in range(NX):
                for y in range(NY):
                    r = x * NY + y
                    gr, er = g[r : r + 1, :], e[r : r + 1, :]
                    vs = [V[full, tile(at(x, c, y))] for c in range(NC)]
                    half = 0.5 * (vs[0] + vs[1] + vs[2])
                    for c in range(NC):
                        k = at(x, c, y)
                        h = H[rows, tile(k)]
                        face = HS[n % 2, rows, X_LO * (1 - x) + X_HI * x + (c * NY + y) * T : X_LO * (1 - x) + X_HI * x + (c * NY + y + 1) * T]
                        near = H[rows, tile(at(1 - x, c, y))] + face
                        y_at = (x * NC + c) * T
                        if y == 0:
                            near = near + HS[n % 2, rows, Y_LO + y_at : Y_LO + y_at + T]
                        else:
                            near = near + H[rows, tile(k - 1)]
                        if y == NY - 1:
                            near = near + HS[n % 2, rows, Y_HI + y_at : Y_HI + y_at + T]
                        else:
                            near = near + H[rows, tile(k + 1)]
                        end = pltpu.roll(ends, (-2 * k) % T, 1) if k else ends
                        near = near + jnp.where(lane == 0, end, pltpu.roll(h, 1, 1))
                        near = near + jnp.where(lane == T - 1, end, pltpu.roll(h, T - 1, 1))
                        kv = gr * (6.0 * h - near) + er * (vs[c] + half)
                        KV[full, tile(k)] = kv
                        if again:
                            OB[block(2 * row + b * 8), tile(k)] = CO[0, r : r + 1, :] * kv
                            w = CO[2, r : r + 1, :] * kv
                            YP[n, rows, tile(k)] = w
                            if y == NY - 1:
                                YK[2 * n + 2, rows, tile(x * NC + c)] = w
                            if y == 0:
                                YK[2 * n + 3, rows, tile(x * NC + c)] = w
                            up = jnp.where(lane == 2 * k, pltpu.roll(w, (2 * k + 1) % T, 1), up)
                            down = jnp.where(lane == (2 * k - 1) % T, pltpu.roll(w, (2 * k - 1) % T, 1), down)
            if again:
                ZK[2 * n + 2, rows, :] = up
                ZK[2 * n + 3, rows, :] = down
            return 0

        lax.fori_loop(0, NV // 8, body, 0)

    def grams(n, part):
        rows = NV * (n + 1)

        def body(j, acc):
            cols = pl.ds(pl.multiple_of(j * CH, CH), CH)
            left = acc[0] + nt(V[0:rows, cols], BR[:, cols])
            return left, acc[1] + nt(KV[0:rows, cols], V[n * NV : rows, cols])

        zero = jnp.zeros((rows, NV), F32)
        left, right = lax.fori_loop(0, COLS // CH, body, (zero, zero))
        part[...] = jnp.concatenate([left, right], axis=1).reshape(part.shape)

    def all_reduce(n, part, a, b, c, d, then):
        def spread(phase, axis, source, place):
            here = me[axis]
            copies = []
            for off in FAR_FIRST[sizes[axis]]:
                to = peer(axis, off)
                copy = remote(source(to), place.at[here], ar_sem.at[n, 0, phase, off], ar_sem.at[n, 1, phase, here], axis, to)
                copy.start()
                copies.append(copy)
            return copies

        def collect(phase, axis, place):
            for off in FAR_FIRST[sizes[axis]]:
                frm = peer(axis, off)
                remote(place.at[frm], place.at[frm], ar_sem.at[n, 0, phase, off], ar_sem.at[n, 1, phase, frm], axis, frm).wait_recv()

        def total(place):
            acc = place[0]
            for i in range(1, place.shape[0]):
                acc = acc + place[i]
            return acc

        copies = spread(0, "gy", lambda to: part.at[to], a)
        a[me["gy"]] = part[me["gy"]]
        collect(0, "gy", a)
        b[me["gx"]] = total(a)
        copies += spread(1, "gx", lambda to: b.at[me["gx"]], b)
        collect(1, "gx", b)
        c[me["gz"]] = total(b)
        copies += spread(2, "gz", lambda to: c.at[me["gz"]], c)
        then()
        collect(2, "gz", c)
        d[me["gy"]] = total(c)
        copies += spread(3, "gy", lambda to: d.at[me["gy"]], d)
        collect(3, "gy", d)
        for copy in copies:
            copy.wait_send()
        return d[...].reshape(-1, T) * (1.0 / dofs)

    def residual(n, coeffs):
        depth = 2 * NV * n
        last = n == 2

        def body(j, _):
            cols = pl.ds(pl.multiple_of(j * CH, CH), CH)
            r = mm(coeffs, OB[0:depth, cols])
            V[n * NV : (n + 1) * NV, cols] = r
            x8 = lax.div(j, NC) * NY
            for y in range(NY):
                part = r[:, tile(y)]
                row = pl.ds(x8 + y, 1)
                here = pl.ds(pl.multiple_of(j * CH + y * T, T), T)
                H[:, here] = g[row, :] * part
                BR[:, here] = rho[row, :] * part
                if not last:
                    OB[depth + NV : depth + 2 * NV, here] = CO[1, row, :] * part
            return 0

        lax.fori_loop(0, COLS // CH, body, 0)

    def residual_halo(n, coeffs):
        depth = 2 * NV * n
        last = n == 2

        def put(cols, q):
            r = mm(coeffs, HB[0:depth, cols])
            HS[n % 2, :, cols] = r
            if not last:
                HB[depth + NV : depth + 2 * NV, cols] = jnp.concatenate([q] * (NV // 8), axis=0) * r

        def body(j, _):
            cols = pl.ds(pl.multiple_of(j * CH, CH), CH)
            put(cols, QH[:, cols])
            return 0

        lax.fori_loop(0, 2 * NC, body, 0)
        put(slice(Y_LO, HALO), QH[:, Y_LO:HALO])

    first[0]()
    first[1]()
    for i, at_x in enumerate((X_LO, X_HI)):
        for c in range(NC):
            QH[:, at_x + c * CH : at_x + (c + 1) * CH] = QX[i]
    for i, at_y in enumerate((Y_LO, Y_HI)):
        HS[0, :, at_y : at_y + EDGE] = YR[i, 0:NV, :]
        QH[:, at_y : at_y + EDGE] = YR[i, NV : NV + 8, :]
    HS[0, :, Z_AT:HALO] = ZR[0, 0, 0:NV, :] + ZR[0, 1, 0:NV, :]
    QH[:, Z_AT:HALO] = ZR[0, 0, NV : NV + 8, :] + ZR[0, 1, NV : NV + 8, :]
    stiffness(0, True)
    grams(0, P0)
    second, third = later(1), later(2)

    def during_first():
        second[0]()
        first[2]()

        def body(b, _):
            for k in range(HALO // T):
                HB[block(NV + b * 8), tile(k)] = QH[:, tile(k)] * HS[0, block(b * 8), tile(k)]
            return 0

        lax.fori_loop(0, NV // 8, body, 0)

    G = all_reduce(0, P0, A0, B0, C0, D0, during_first)
    li0 = factor_inverse(G[:, :NV])
    theta0 = nt(mm(li0, G[:, NV:]), li0)
    c0 = jnp.concatenate([li0, -mm(theta0, li0)], axis=1)
    SM[0], SM[1] = li0, theta0
    residual(1, c0)
    second[1]()
    HB[0:NV, Z_AT:HALO] = ZR[1, 0, 0:NV, :] + ZR[1, 1, 0:NV, :]
    residual_halo(1, c0)
    stiffness(1, True)
    grams(1, P1)

    G = all_reduce(1, P1, A1, B1, C1, D1, third[0])
    li0, theta0 = SM[0], SM[1]
    cross = mm(li0, G[:NV, :])
    mxr, kxr = cross[:, :NV], cross[:, NV:]
    li_r = factor_inverse(G[NV:, :NV] - tn(mxr, mxr))
    li = jnp.concatenate(
        [jnp.concatenate([one, zero], axis=1), jnp.concatenate([-nt(li_r, mxr), li_r], axis=1)], axis=0
    )
    ga = jnp.concatenate(
        [jnp.concatenate([theta0, kxr], axis=1), jnp.concatenate([kxr.T, G[NV:, NV:]], axis=1)], axis=0
    )
    h = nt(mm(li, ga), li)
    qt, th, theta1 = filtered(h)
    ct = mm(qt, li)
    a2t = ct[:, NV:]
    a1t = mm(ct[:, :NV], li0)
    c1 = jnp.concatenate([a1t, -mm(theta1, a1t), a2t, -mm(theta1, a2t)], axis=1)
    ut = jnp.concatenate([nt(a2t, mxr), qt[:, NV:]], axis=1)
    SM[2], SM[3], SM[4] = theta1, a1t, a2t
    mxp, mpp = nt(qt, ut), nt(ut, ut)
    SM[5], SM[6], SM[7], SM[8] = mxp, mpp - tn(mxp, mxp), nt(th, ut), nt(mm(ut, h), ut)
    residual(2, c1)
    third[1]()
    HB[2 * NV : 3 * NV, Z_AT:HALO] = ZR[2, 0, 0:NV, :] + ZR[2, 1, 0:NV, :]
    residual_halo(2, c1)
    stiffness(2, False)
    grams(2, P2)

    G = all_reduce(2, P2, A2, B2, C2, D2, lambda: None)
    theta1, a1t, a2t, mxp, spp, kxp, kpp = (SM[i] for i in range(2, 9))
    cross_p = mm(a2t, G[NV : 2 * NV, :])
    cross = mm(jnp.concatenate([a1t, a2t], axis=1), G[: 2 * NV, :])
    mxr, kxr = cross[:, :NV], cross[:, NV:]
    mpr, kpr = cross_p[:, :NV], cross_p[:, NV:]
    li_r = factor_inverse(G[2 * NV :, :NV] - tn(mxr, mxr))
    l32 = nt(mpr - tn(mxp, mxr), li_r)
    li_p = factor_inverse(spp - nt(l32, l32))
    below = -nt(li_r, mxr)
    li = jnp.concatenate(
        [
            jnp.concatenate([one, zero, zero], axis=1),
            jnp.concatenate([below, li_r, zero], axis=1),
            jnp.concatenate([mm(li_p, -mxp.T - mm(l32, below)), -mm(li_p, mm(l32, li_r)), li_p], axis=1),
        ],
        axis=0,
    )
    ga = jnp.concatenate(
        [
            jnp.concatenate([theta1, kxr, kxp], axis=1),
            jnp.concatenate([kxr.T, G[2 * NV :, NV:], kpr.T], axis=1),
            jnp.concatenate([kxp.T, kpr, kpp], axis=1),
        ],
        axis=0,
    )
    h = nt(mm(li, ga), li)
    qt, th, theta2 = filtered(h)
    ritz[...] = theta2
    ct = mm(qt, li)
    ft = jnp.concatenate(
        [mm(ct[:, :NV], a1t), mm(ct[:, :NV] + ct[:, 2 * NV :], a2t), ct[:, NV : 2 * NV]], axis=1
    )

    for j in range(COLS // CH):
        x, c = divmod(j, NC)
        modes = mm(ft, V[:, j * CH : (j + 1) * CH])
        for y in range(NY):
            for b in range(NV // 8):
                out[pl.ds(b * 384 + (c * NX + x) * NY + y, 8, stride=48), :] = modes[8 * b : 8 * b + 8, tile(y)]

    second[2]()
    third[2]()


def local(sizes, start_block, stiff_field, shift_field, mass_field):
    dofs = 3.0 * stiff_field.size * sizes["gx"] * sizes["gy"] * sizes["gz"]
    rows = NX * NY
    scratch = [
        pltpu.VMEM((3 * NV, COLS), F32),
        pltpu.VMEM((3 * NV, COLS), F32),
        pltpu.VMEM((NV, COLS), F32),
        pltpu.VMEM((NV, COLS), F32),
        pltpu.VMEM((4 * NV, COLS), F32),
        pltpu.VMEM((4 * NV, HALO), F32),
        pltpu.VMEM((2, NV, HALO), F32),
        pltpu.VMEM((8, 2 * CH), F32),
        pltpu.VMEM((2, 8, CH), F32),
        pltpu.VMEM((8, HALO), F32),
        pltpu.VMEM((2, NV, COLS), F32),
        pltpu.VMEM((6, NV + 8, EDGE), F32),
        pltpu.VMEM((2, NV + 8, EDGE), F32),
        pltpu.VMEM((6, NV + 8, T), F32),
        pltpu.VMEM((3, 2, NV + 8, T), F32),
        pltpu.VMEM((3, rows, T), F32),
    ]
    heights = [NV * (i + 1) // 8 for i in range(3)]
    for lead in (8, sizes["gy"], sizes["gx"], sizes["gz"], 8):
        scratch += [pltpu.VMEM((lead, h, T), F32) for h in heights]
    scratch += [pltpu.VMEM((9, NV, NV), F32)]
    scratch += [pltpu.SemaphoreType.DMA((3, 2, 4, 8)), pltpu.SemaphoreType.DMA((3, 2, 8))]
    vmem = pl.BlockSpec(memory_space=pltpu.VMEM)
    modes, ritz = pl.pallas_call(
        functools.partial(kernel, dofs, sizes),
        out_shape=(
            jax.ShapeDtypeStruct((start_block.size // T, T), F32),
            jax.ShapeDtypeStruct((NV, NV), F32),
        ),
        in_specs=[vmem] * 4,
        out_specs=(vmem, vmem),
        scratch_shapes=scratch,
        compiler_params=pltpu.CompilerParams(
            collective_id=0, has_side_effects=True, vmem_limit_bytes=62 * 1024 * 1024
        ),
        name="lobpcg",
    )(
        start_block.reshape(-1, T),
        stiff_field.reshape(rows, T),
        shift_field.reshape(rows, T),
        mass_field.reshape(rows, T),
    )
    return modes.reshape(start_block.shape), ritz


def solution(mesh):
    field = P("gx", "gy", "gz")
    block = P(None, None, "gx", "gy", "gz")
    return jax.shard_map(
        functools.partial(local, dict(mesh.shape)),
        mesh=mesh,
        in_specs=(block, field, field, field),
        out_specs=(block, P()),
        check_vma=False,
    )
```

profile of v0, /device:TPU:1, one launch (start us, length us, event | category | flops | bytes accessed | tf_op | source)
XLA Modules:
  0.0 172.9 jit_solution(4934501131785555973)
XLA Ops:
  0.6 169.0 %lobpcg.1 = (f32[3072,128]{1,0:T(8,128)}, f32[64,64]{1,0:T(8,128)}) custom-call(f32[3072,128]{1,0:T(8,128)} %bitcast.5, f32[16,128]{1,0:T(8,128)} %bitcast.7, f32[16,128]{1,0:T(8,128)} %bitcast.8, f32[16,128]{1,0:T(8,128)} %bitcast.9), custom_call_target="tpu_custom_call" | custom-call | tf_op jit(solution)/shard_map/lobpcg/pallas_call | solution.py:522
  169.6 0.0 copy-start
  169.6 2.7 %copy.8 = f32[64,3,2,8,128]{4,3,2,1,0:T(8,128)} copy(f32[64,3,2,8,128]{4,3,2,1,0:T(8,128)} %bitcast.6) | data formatting | bytes 3145728
  172.3 0.0 copy-done
  172.3 0.6 copy.9
Async XLA Ops:
  169.6 2.7 %copy-start = (f32[64,64]{1,0:T(8,128)S(1)}, f32[64,64]{1,0:T(8,128)}, u32[]{:S(2)}) copy-start(f32[64,64]{1,0:T(8,128)} %get-tuple-element.9) | copy-start | bytes 49156
where the time goes:
time: 173 us
  Pallas kernels  169 us (98%)
  local copies, waits for them, and re-layouts  3.28 us (2%)
    pallas_call x1, Pallas kernels, local(): pl.pallas_call(functools.partial(kernel, dofs, sizes), out_shape=(jax.Sha...  169 us

commit v1 on v0

--- a/solution.py
+++ b/solution.py
@@ -18,6 +18,7 @@
 X_LO, X_HI = 0, PLANE
 Y_LO, Y_HI = 2 * PLANE, 2 * PLANE + EDGE
 Z_AT = 2 * PLANE + 2 * EDGE
+STEP = 16
 HALO = Z_AT + T
 CH = NY * T
 FAR_FIRST = {4: (2, 1, 3), 8: (4, 3, 5, 2, 6, 1, 7)}
@@ -35,6 +36,18 @@
 
 def tn(a, b):
     return mm(a, b, 0, 0)
+
+
+def parts_of(x):
+    high = x.astype(jnp.bfloat16)
+    return high, (x - high.astype(F32)).astype(jnp.bfloat16)
+
+
+def dot3(a, b, cb=0):
+    dims = (((1,), (cb,)), ((), ()))
+    small = lax.dot_general(a[1], b[0], dims, preferred_element_type=F32)
+    small = small + lax.dot_general(a[0], b[1], dims, preferred_element_type=F32)
+    return lax.dot_general(a[0], b[0], dims, preferred_element_type=F32) + small
 
 
 def eye(n):
@@ -113,12 +126,16 @@
 def kernel(
     dofs, sizes,
     s, g, e, rho, out, ritz,
-    V, KV, H, BR, OB, HB, HS, QF, QX, QH, YP, YK, YR, ZK, ZR, CO,
+    V, VP, KP, H, BP, OP, HB, HS, CF, QX, QH, YP, YK, YR, ZK, ZR,
     P0, P1, P2, A0, A1, A2, B0, B1, B2, C0, C1, C2, D0, D1, D2,
-    SM, ar_sem, halo_sem,
+    SM, SQ, SH, ar_sem, halo_sem,
 ):
     me = {a: lax.axis_index(a) for a in ("gx", "gy", "gz")}
     lane = lax.broadcasted_iota(jnp.int32, (8, T), 1)
+    lane_s = lax.broadcasted_iota(jnp.int32, (STEP, T), 1)
+
+    def keep(ref, rows, cols, value):
+        ref[0, rows, cols], ref[1, rows, cols] = parts_of(value)
 
     def peer(axis, off):
         return lax.rem(me[axis] + off, sizes[axis])
@@ -145,41 +162,45 @@
 
     diag = 6.0 * g[...] * g[...] + 1.5 * e[...]
     inv = 1.0 / diag
-    CO[0] = inv
-    CO[1] = rho[...] * inv
-    CO[2] = g[...] * inv
+    for i, field in enumerate((g[...], e[...], rho[...], inv, rho[...] * inv, g[...] * inv)):
+        for r in range(NX * NY):
+            CF[i, :, tile(r)] = jnp.broadcast_to(field[r : r + 1, :], (8, T))
+    G_, E_, RHO, INV, Q, GINV = range(6)
+
+    def coef(i, r, n=STEP):
+        return jnp.concatenate([CF[i, :, tile(r)]] * (n // 8), axis=0)
 
     def load(b, _):
-        up, down = jnp.zeros((8, T), F32), jnp.zeros((8, T), F32)
-        rows = block(b * 8)
+        up, down = jnp.zeros((STEP, T), F32), jnp.zeros((STEP, T), F32)
+        rows = block(b * STEP, STEP)
         for x in range(NX):
             for y in range(NY):
                 r = x * NY + y
-                gr, qr, mr = g[r : r + 1, :], CO[1, r : r + 1, :], rho[r : r + 1, :]
+                gr, qr, mr = coef(G_, r), coef(Q, r), coef(RHO, r)
                 for c in range(NC):
                     k = at(x, c, y)
-                    v = s[pl.ds(b * 384 + (c * NX + x) * NY + y, 8, stride=48), :]
+                    v = s[pl.ds(b * (48 * STEP) + (c * NX + x) * NY + y, STEP, stride=48), :]
                     h = gr * v
                     V[rows, tile(k)] = v
+                    keep(VP, rows, tile(k), v)
                     H[rows, tile(k)] = h
-                    BR[rows, tile(k)] = mr * v
-                    OB[block(NV + b * 8), tile(k)] = qr * v
+                    keep(BP, rows, tile(k), mr * v)
+                    keep(OP, block(NV + b * STEP, STEP), tile(k), qr * v)
                     if y == NY - 1:
                         YK[0, rows, tile(x * NC + c)] = h
                     if y == 0:
                         YK[1, rows, tile(x * NC + c)] = h
-                    up = jnp.where(lane == 2 * k, pltpu.roll(h, (2 * k + 1) % T, 1), up)
-                    down = jnp.where(lane == (2 * k - 1) % T, pltpu.roll(h, (2 * k - 1) % T, 1), down)
+                    up = jnp.where(lane_s == 2 * k, pltpu.roll(h, (2 * k + 1) % T, 1), up)
+                    down = jnp.where(lane_s == (2 * k - 1) % T, pltpu.roll(h, (2 * k - 1) % T, 1), down)
         ZK[0, rows, :] = up
         ZK[1, rows, :] = down
         return 0
 
-    lax.fori_loop(0, NV // 8, load, 0)
+    lax.fori_loop(0, NV // STEP, load, 0)
     up, down = jnp.zeros((8, T), F32), jnp.zeros((8, T), F32)
     for x in range(NX):
         for y in range(NY):
-            q = jnp.broadcast_to(CO[1, x * NY + y : x * NY + y + 1, :], (8, T))
-            QF[:, tile(x * NY + y)] = q
+            q = CF[Q, :, tile(x * NY + y)]
             for c in range(NC):
                 k = at(x, c, y)
                 if y == NY - 1:
@@ -229,80 +250,116 @@
 
     first = exchange(0, [
         ("gx", H.at[:, PLANE:COLS], H.at[:, 0:PLANE], HS.at[0, :, X_LO : X_LO + PLANE], HS.at[0, :, X_HI : X_HI + PLANE]),
-        ("gx", QF.at[:, CH : 2 * CH], QF.at[:, 0:CH], QX.at[0], QX.at[1]),
+        ("gx", CF.at[Q, :, CH : 2 * CH], CF.at[Q, :, 0:CH], QX.at[0], QX.at[1]),
         ("gy", YK.at[0], YK.at[1], YR.at[0], YR.at[1]),
         ("gz", ZK.at[0], ZK.at[1], ZR.at[0, 0], ZR.at[0, 1]),
     ])
 
     def later(n):
-        top = 2 * NV * (n - 1)
+        top, cut = 2 * NV * (n - 1), 8 * (n + 2)
         row = pl.ds(top, NV)
-        return exchange(n, [
+
+        def x_faces(a, b):
+            mine, theirs = pl.ds(a, b - a), pl.ds(top + a, b - a)
+            return (
+                "gx", YP.at[n - 1, mine, PLANE:COLS], YP.at[n - 1, mine, 0:PLANE],
+                HB.at[theirs, X_LO : X_LO + PLANE], HB.at[theirs, X_HI : X_HI + PLANE],
+            )
+
+        early = exchange(3 * n - 2, [x_faces(0, cut)])
+        rest = exchange(3 * n - 1, [x_faces(cut, NV)])
+        ends = exchange(3 * n, [
             ("gz", ZK.at[2 * n, 0:NV], ZK.at[2 * n + 1, 0:NV], ZR.at[n, 0, 0:NV], ZR.at[n, 1, 0:NV]),
             ("gy", YK.at[2 * n, 0:NV], YK.at[2 * n + 1, 0:NV], HB.at[row, Y_LO : Y_LO + EDGE], HB.at[row, Y_HI : Y_HI + EDGE]),
-            ("gx", YP.at[n - 1, :, PLANE:COLS], YP.at[n - 1, :, 0:PLANE], HB.at[row, X_LO : X_LO + PLANE], HB.at[row, X_HI : X_HI + PLANE]),
         ])
+
+        def others():
+            rest[0]()
+            pack_ends(n - 1)
+            ends[0]()
+
+        def every(k):
+            for part in (early, ends, rest):
+                part[k]()
+
+        return early[0], others, functools.partial(every, 1), functools.partial(every, 2)
+
+    def pack_ends(n):
+        def body(b, _):
+            rows = block(b * 8)
+            up, down = jnp.zeros((8, T), F32), jnp.zeros((8, T), F32)
+            for k in range(COLS // T):
+                w = YP[n, rows, tile(k)]
+                up = jnp.where(lane == 2 * k, pltpu.roll(w, (2 * k + 1) % T, 1), up)
+                down = jnp.where(lane == (2 * k - 1) % T, pltpu.roll(w, (2 * k - 1) % T, 1), down)
+            ZK[2 * n + 2, rows, :] = up
+            ZK[2 * n + 3, rows, :] = down
+            return 0
+
+        lax.fori_loop(0, NV // 8, body, 0)
 
     def stiffness(n, again):
         row = n * NV
 
         def body(b, _):
-            up, down = jnp.zeros((8, T), F32), jnp.zeros((8, T), F32)
-            rows, full = block(b * 8), block(row + b * 8)
+            rows, full = block(b * STEP, STEP), block(row + b * STEP, STEP)
             ends = HS[n % 2, rows, Z_AT:HALO]
-            for x in range(NX):
-                for y in range(NY):
+            held = {}
+
+            def h_at(x, c, y):
+                if (x, c, y) not in held:
+                    if y < 0:
+                        held[x, c, y] = HS[n % 2, rows, Y_LO + (x * NC + c) * T : Y_LO + (x * NC + c + 1) * T]
+                    elif y == NY:
+                        held[x, c, y] = HS[n % 2, rows, Y_HI + (x * NC + c) * T : Y_HI + (x * NC + c + 1) * T]
+                    else:
+                        held[x, c, y] = H[rows, tile(at(x, c, y))]
+                return held[x, c, y]
+
+            for y in range(NY):
+                for x in range(NX):
                     r = x * NY + y
-                    gr, er = g[r : r + 1, :], e[r : r + 1, :]
-                    vs = [V[full, tile(at(x, c, y))] for c in range(NC)]
+                    gr, er = coef(G_, r), coef(E_, r)
+                    vs = [V[rows, tile(at(x, c, y))] for c in range(NC)]
                     half = 0.5 * (vs[0] + vs[1] + vs[2])
                     for c in range(NC):
                         k = at(x, c, y)
-                        h = H[rows, tile(k)]
-                        face = HS[n % 2, rows, X_LO * (1 - x) + X_HI * x + (c * NY + y) * T : X_LO * (1 - x) + X_HI * x + (c * NY + y + 1) * T]
-                        near = H[rows, tile(at(1 - x, c, y))] + face
-                        y_at = (x * NC + c) * T
-                        if y == 0:
-                            near = near + HS[n % 2, rows, Y_LO + y_at : Y_LO + y_at + T]
-                        else:
-                            near = near + H[rows, tile(k - 1)]
-                        if y == NY - 1:
-                            near = near + HS[n % 2, rows, Y_HI + y_at : Y_HI + y_at + T]
-                        else:
-                            near = near + H[rows, tile(k + 1)]
+                        h = h_at(x, c, y)
+                        face = (X_HI if x else X_LO) + (c * NY + y) * T
+                        near = h_at(1 - x, c, y) + HS[n % 2, rows, face : face + T]
+                        near = near + h_at(x, c, y - 1) + h_at(x, c, y + 1)
                         end = pltpu.roll(ends, (-2 * k) % T, 1) if k else ends
-                        near = near + jnp.where(lane == 0, end, pltpu.roll(h, 1, 1))
-                        near = near + jnp.where(lane == T - 1, end, pltpu.roll(h, T - 1, 1))
+                        near = near + jnp.where(lane_s == 0, end, pltpu.roll(h, 1, 1))
+                        near = near + jnp.where(lane_s == T - 1, end, pltpu.roll(h, T - 1, 1))
                         kv = gr * (6.0 * h - near) + er * (vs[c] + half)
-                        KV[full, tile(k)] = kv
+                        keep(KP, full, tile(k), kv)
                         if again:
-                            OB[block(2 * row + b * 8), tile(k)] = CO[0, r : r + 1, :] * kv
-                            w = CO[2, r : r + 1, :] * kv
+                            keep(OP, block(2 * row + b * STEP, STEP), tile(k), coef(INV, r) * kv)
+                            w = coef(GINV, r) * kv
                             YP[n, rows, tile(k)] = w
                             if y == NY - 1:
                                 YK[2 * n + 2, rows, tile(x * NC + c)] = w
                             if y == 0:
                                 YK[2 * n + 3, rows, tile(x * NC + c)] = w
-                            up = jnp.where(lane == 2 * k, pltpu.roll(w, (2 * k + 1) % T, 1), up)
-                            down = jnp.where(lane == (2 * k - 1) % T, pltpu.roll(w, (2 * k - 1) % T, 1), down)
-            if again:
-                ZK[2 * n + 2, rows, :] = up
-                ZK[2 * n + 3, rows, :] = down
             return 0
 
-        lax.fori_loop(0, NV // 8, body, 0)
-
-    def grams(n, part):
+        lax.fori_loop(0, NV // STEP, body, 0)
+
+    def gram(n, mass, part):
         rows = NV * (n + 1)
+        left, right, first_row = (VP, BP, 0) if mass else (KP, VP, n * NV)
 
         def body(j, acc):
             cols = pl.ds(pl.multiple_of(j * CH, CH), CH)
-            left = acc[0] + nt(V[0:rows, cols], BR[:, cols])
-            return left, acc[1] + nt(KV[0:rows, cols], V[n * NV : rows, cols])
-
-        zero = jnp.zeros((rows, NV), F32)
-        left, right = lax.fori_loop(0, COLS // CH, body, (zero, zero))
-        part[...] = jnp.concatenate([left, right], axis=1).reshape(part.shape)
+            return acc + dot3(
+                [left[i, 0:rows, cols] for i in range(2)],
+                [right[i, first_row : first_row + NV, cols] for i in range(2)],
+                1,
+            )
+
+        total = lax.fori_loop(0, COLS // CH, body, jnp.zeros((rows, NV), F32))
+        lanes = slice(0, NV) if mass else slice(NV, 2 * NV)
+        part[:, :, lanes] = total.reshape(part.shape[0], part.shape[1], NV)
 
     def all_reduce(n, part, a, b, c, d, then):
         def spread(phase, axis, source, place):
@@ -346,20 +403,26 @@
     def residual(n, coeffs):
         depth = 2 * NV * n
         last = n == 2
+        own = slice(n * NV, (n + 1) * NV)
 
         def body(j, _):
             cols = pl.ds(pl.multiple_of(j * CH, CH), CH)
-            r = mm(coeffs, OB[0:depth, cols])
-            V[n * NV : (n + 1) * NV, cols] = r
+            r = dot3(coeffs, [OP[i, 0:depth, cols] for i in range(2)])
+            V[:, cols] = r
+            keep(VP, own, cols, r)
             x8 = lax.div(j, NC) * NY
             for y in range(NY):
                 part = r[:, tile(y)]
-                row = pl.ds(x8 + y, 1)
+                row = pl.ds(pl.multiple_of((x8 + y) * T, T), T)
+
+                def field(i):
+                    return jnp.concatenate([CF[i, :, row]] * (NV // 8), axis=0)
+
                 here = pl.ds(pl.multiple_of(j * CH + y * T, T), T)
-                H[:, here] = g[row, :] * part
-                BR[:, here] = rho[row, :] * part
+                H[:, here] = field(G_) * part
+                keep(BP, slice(0, NV), here, field(RHO) * part)
                 if not last:
-                    OB[depth + NV : depth + 2 * NV, here] = CO[1, row, :] * part
+                    keep(OP, slice(depth + NV, depth + 2 * NV), here, field(Q) * part)
             return 0
 
         lax.fori_loop(0, COLS // CH, body, 0)
@@ -369,7 +432,7 @@
         last = n == 2
 
         def put(cols, q):
-            r = mm(coeffs, HB[0:depth, cols])
+            r = dot3(coeffs, parts_of(HB[0:depth, cols]))
             HS[n % 2, :, cols] = r
             if not last:
                 HB[depth + NV : depth + 2 * NV, cols] = jnp.concatenate([q] * (NV // 8), axis=0) * r
@@ -383,6 +446,7 @@
         put(slice(Y_LO, HALO), QH[:, Y_LO:HALO])
 
     first[0]()
+    gram(0, True, P0)
     first[1]()
     for i, at_x in enumerate((X_LO, X_HI)):
         for c in range(NC):
@@ -393,11 +457,12 @@
     HS[0, :, Z_AT:HALO] = ZR[0, 0, 0:NV, :] + ZR[0, 1, 0:NV, :]
     QH[:, Z_AT:HALO] = ZR[0, 0, NV : NV + 8, :] + ZR[0, 1, NV : NV + 8, :]
     stiffness(0, True)
-    grams(0, P0)
     second, third = later(1), later(2)
+    second[0]()
+    gram(0, False, P0)
 
     def during_first():
-        second[0]()
+        second[1]()
         first[2]()
 
         def body(b, _):
@@ -410,16 +475,18 @@
     G = all_reduce(0, P0, A0, B0, C0, D0, during_first)
     li0 = factor_inverse(G[:, :NV])
     theta0 = nt(mm(li0, G[:, NV:]), li0)
-    c0 = jnp.concatenate([li0, -mm(theta0, li0)], axis=1)
+    c0 = parts_of(jnp.concatenate([li0, -mm(theta0, li0)], axis=1))
     SM[0], SM[1] = li0, theta0
     residual(1, c0)
-    second[1]()
+    gram(1, True, P1)
+    second[2]()
     HB[0:NV, Z_AT:HALO] = ZR[1, 0, 0:NV, :] + ZR[1, 1, 0:NV, :]
     residual_halo(1, c0)
     stiffness(1, True)
-    grams(1, P1)
-
-    G = all_reduce(1, P1, A1, B1, C1, D1, third[0])
+    third[0]()
+    gram(1, False, P1)
+
+    G = all_reduce(1, P1, A1, B1, C1, D1, third[1])
     li0, theta0 = SM[0], SM[1]
     cross = mm(li0, G[:NV, :])
     mxr, kxr = cross[:, :NV], cross[:, NV:]
@@ -435,20 +502,25 @@
     ct = mm(qt, li)
     a2t = ct[:, NV:]
     a1t = mm(ct[:, :NV], li0)
-    c1 = jnp.concatenate([a1t, -mm(theta1, a1t), a2t, -mm(theta1, a2t)], axis=1)
-    ut = jnp.concatenate([nt(a2t, mxr), qt[:, NV:]], axis=1)
-    SM[2], SM[3], SM[4] = theta1, a1t, a2t
-    mxp, mpp = nt(qt, ut), nt(ut, ut)
-    SM[5], SM[6], SM[7], SM[8] = mxp, mpp - tn(mxp, mxp), nt(th, ut), nt(mm(ut, h), ut)
+    c1 = parts_of(jnp.concatenate([a1t, -mm(theta1, a1t), a2t, -mm(theta1, a2t)], axis=1))
+    SM[2], SM[3], SM[4], SM[5] = theta1, a1t, a2t, mxr
+    SQ[0], SQ[1], SH[...] = qt, th, h
     residual(2, c1)
-    third[1]()
+    gram(2, True, P2)
+    third[2]()
     HB[2 * NV : 3 * NV, Z_AT:HALO] = ZR[2, 0, 0:NV, :] + ZR[2, 1, 0:NV, :]
     residual_halo(2, c1)
     stiffness(2, False)
-    grams(2, P2)
-
-    G = all_reduce(2, P2, A2, B2, C2, D2, lambda: None)
-    theta1, a1t, a2t, mxp, spp, kxp, kpp = (SM[i] for i in range(2, 9))
+    gram(2, False, P2)
+
+    def during_third():
+        qt, th = SQ[0], SQ[1]
+        ut = jnp.concatenate([nt(SM[4], SM[5]), qt[:, NV:]], axis=1)
+        mxp, mpp = nt(qt, ut), nt(ut, ut)
+        SM[6], SM[7], SM[8], SM[9] = mxp, mpp - tn(mxp, mxp), nt(th, ut), nt(mm(ut, SH[...]), ut)
+
+    G = all_reduce(2, P2, A2, B2, C2, D2, during_third)
+    theta1, a1t, a2t, _, mxp, spp, kxp, kpp = (SM[i] for i in range(2, 10))
     cross_p = mm(a2t, G[NV : 2 * NV, :])
     cross = mm(jnp.concatenate([a1t, a2t], axis=1), G[: 2 * NV, :])
     mxr, kxr = cross[:, :NV], cross[:, NV:]
@@ -477,33 +549,36 @@
     qt, th, theta2 = filtered(h)
     ritz[...] = theta2
     ct = mm(qt, li)
-    ft = jnp.concatenate(
-        [mm(ct[:, :NV], a1t), mm(ct[:, :NV] + ct[:, 2 * NV :], a2t), ct[:, NV : 2 * NV]], axis=1
+    ft = parts_of(
+        jnp.concatenate(
+            [mm(ct[:, :NV], a1t), mm(ct[:, :NV] + ct[:, 2 * NV :], a2t), ct[:, NV : 2 * NV]], axis=1
+        )
     )
 
     for j in range(COLS // CH):
         x, c = divmod(j, NC)
-        modes = mm(ft, V[:, j * CH : (j + 1) * CH])
+        modes = dot3(ft, [VP[i, :, j * CH : (j + 1) * CH] for i in range(2)])
         for y in range(NY):
             for b in range(NV // 8):
                 out[pl.ds(b * 384 + (c * NX + x) * NY + y, 8, stride=48), :] = modes[8 * b : 8 * b + 8, tile(y)]
 
-    second[2]()
-    third[2]()
+    second[3]()
+    third[3]()
 
 
 def local(sizes, start_block, stiff_field, shift_field, mass_field):
     dofs = 3.0 * stiff_field.size * sizes["gx"] * sizes["gy"] * sizes["gz"]
     rows = NX * NY
     scratch = [
-        pltpu.VMEM((3 * NV, COLS), F32),
-        pltpu.VMEM((3 * NV, COLS), F32),
         pltpu.VMEM((NV, COLS), F32),
+        pltpu.VMEM((2, 3 * NV, COLS), jnp.bfloat16),
+        pltpu.VMEM((2, 3 * NV, COLS), jnp.bfloat16),
         pltpu.VMEM((NV, COLS), F32),
-        pltpu.VMEM((4 * NV, COLS), F32),
+        pltpu.VMEM((2, NV, COLS), jnp.bfloat16),
+        pltpu.VMEM((2, 4 * NV, COLS), jnp.bfloat16),
         pltpu.VMEM((4 * NV, HALO), F32),
         pltpu.VMEM((2, NV, HALO), F32),
-        pltpu.VMEM((8, 2 * CH), F32),
+        pltpu.VMEM((6, 8, 2 * CH), F32),
         pltpu.VMEM((2, 8, CH), F32),
         pltpu.VMEM((8, HALO), F32),
         pltpu.VMEM((2, NV, COLS), F32),
@@ -511,13 +586,13 @@
         pltpu.VMEM((2, NV + 8, EDGE), F32),
         pltpu.VMEM((6, NV + 8, T), F32),
         pltpu.VMEM((3, 2, NV + 8, T), F32),
-        pltpu.VMEM((3, rows, T), F32),
     ]
     heights = [NV * (i + 1) // 8 for i in range(3)]
     for lead in (8, sizes["gy"], sizes["gx"], sizes["gz"], 8):
         scratch += [pltpu.VMEM((lead, h, T), F32) for h in heights]
-    scratch += [pltpu.VMEM((9, NV, NV), F32)]
-    scratch += [pltpu.SemaphoreType.DMA((3, 2, 4, 8)), pltpu.SemaphoreType.DMA((3, 2, 8))]
+    scratch += [pltpu.VMEM((10, NV, NV), F32)]
+    scratch += [pltpu.VMEM((2, NV, 2 * NV), F32), pltpu.VMEM((2 * NV, 2 * NV), F32)]
+    scratch += [pltpu.SemaphoreType.DMA((3, 2, 4, 8)), pltpu.SemaphoreType.DMA((7, 2, 8))]
     vmem = pl.BlockSpec(memory_space=pltpu.VMEM)
     modes, ritz = pl.pallas_call(
         functools.partial(kernel, dofs, sizes),

time: 173 us -> 135 us (0.78)
  Pallas kernels: 169 us -> 131 us
    pallas_call x1, Pallas kernels: 169 us -> 131 us  [local(): pl.pallas_call(functools.partial(kernel, dofs, sizes), out_shape=(jax.Sha...]
where the time goes in v1:
time: 135 us
  Pallas kernels  131 us (97%)
  local copies, waits for them, and re-layouts  3.28 us (2%)
    pallas_call x1, Pallas kernels, local(): pl.pallas_call(functools.partial(kernel, dofs, sizes), out_shape=(jax.Sha...  131 us
    unnamed x4, local copies, waits for them, and re-layouts  3.28 us

profile of v1, /device:TPU:1, one launch (start us, length us, event | category | flops | bytes accessed | tf_op | source)
XLA Modules:
  0.0 134.8 jit_solution(1261961533806210712)
XLA Ops:
  0.6 130.9 %lobpcg.1 = (f32[3072,128]{1,0:T(8,128)}, f32[64,64]{1,0:T(8,128)}) custom-call(f32[3072,128]{1,0:T(8,128)} %bitcast.5, f32[16,128]{1,0:T(8,128)} %bitcast.7, f32[16,128]{1,0:T(8,128)} %bitcast.8, f32[16,128]{1,0:T(8,128)} %bitcast.9), custom_call_target="tpu_custom_call" | custom-call | tf_op jit(solution)/shard_map/lobpcg/pallas_call | solution.py:597
  131.5 0.0 copy-start
  131.5 2.7 %copy.8 = f32[64,3,2,8,128]{4,3,2,1,0:T(8,128)} copy(f32[64,3,2,8,128]{4,3,2,1,0:T(8,128)} %bitcast.6) | data formatting | bytes 3145728
  134.2 0.0 copy-done
  134.2 0.6 copy.9
Async XLA Ops:
  131.5 2.7 %copy-start = (f32[64,64]{1,0:T(8,128)S(1)}, f32[64,64]{1,0:T(8,128)}, u32[]{:S(2)}) copy-start(f32[64,64]{1,0:T(8,128)} %get-tuple-element.9) | copy-start | bytes 49156

commit v2 on v1

--- a/solution.py
+++ b/solution.py
@@ -127,9 +127,9 @@
     dofs, sizes,
     s, g, e, rho, out, ritz,
     V, VP, KP, H, BP, OP, HB, HS, CF, QX, QH, YP, YK, YR, ZK, ZR,
-    P0, P1, P2, A0, A1, A2, B0, B1, B2, C0, C1, C2, D0, D1, D2,
-    SM, SQ, SH, ar_sem, halo_sem,
+    *rest,
 ):
+    sums, (SM, SQ, SH, ar_sem, halo_sem) = [rest[i : i + 5] for i in range(0, 30, 5)], rest[30:]
     me = {a: lax.axis_index(a) for a in ("gx", "gy", "gz")}
     lane = lax.broadcasted_iota(jnp.int32, (8, T), 1)
     lane_s = lax.broadcasted_iota(jnp.int32, (STEP, T), 1)
@@ -256,7 +256,7 @@
     ])
 
     def later(n):
-        top, cut = 2 * NV * (n - 1), 8 * (n + 2)
+        top, cut = 2 * NV * (n - 1), 8 * (n + 1)
         row = pl.ds(top, NV)
 
         def x_faces(a, b):
@@ -351,17 +351,20 @@
 
         def body(j, acc):
             cols = pl.ds(pl.multiple_of(j * CH, CH), CH)
-            return acc + dot3(
-                [left[i, 0:rows, cols] for i in range(2)],
-                [right[i, first_row : first_row + NV, cols] for i in range(2)],
-                1,
-            )
+            big, small = left[0, 0:rows, cols], left[1, 0:rows, cols]
+            pair = [right[i, first_row : first_row + NV, cols] for i in range(2)]
+            dims = (((1,), (1,)), ((), ()))
+            both = lax.dot_general(jnp.concatenate([big, small], axis=0), pair[0], dims, preferred_element_type=F32)
+            last = lax.dot_general(big, pair[1], dims, preferred_element_type=F32)
+            return acc + both[:rows] + (both[rows:] + last)
 
         total = lax.fori_loop(0, COLS // CH, body, jnp.zeros((rows, NV), F32))
-        lanes = slice(0, NV) if mass else slice(NV, 2 * NV)
-        part[:, :, lanes] = total.reshape(part.shape[0], part.shape[1], NV)
-
-    def all_reduce(n, part, a, b, c, d, then):
+        part[...] = jnp.concatenate([total, total], axis=1).reshape(part.shape)
+
+    def reducer(n):
+        part, a, b, c, d = sums[n]
+        copies = []
+
         def spread(phase, axis, source, place):
             here = me[axis]
             copies = []
@@ -383,22 +386,32 @@
                 acc = acc + place[i]
             return acc
 
-        copies = spread(0, "gy", lambda to: part.at[to], a)
-        a[me["gy"]] = part[me["gy"]]
-        collect(0, "gy", a)
-        b[me["gx"]] = total(a)
-        copies += spread(1, "gx", lambda to: b.at[me["gx"]], b)
-        collect(1, "gx", b)
-        c[me["gz"]] = total(b)
-        copies += spread(2, "gz", lambda to: c.at[me["gz"]], c)
-        then()
-        collect(2, "gz", c)
-        d[me["gy"]] = total(c)
-        copies += spread(3, "gy", lambda to: d.at[me["gy"]], d)
-        collect(3, "gy", d)
-        for copy in copies:
-            copy.wait_send()
-        return d[...].reshape(-1, T) * (1.0 / dofs)
+        def step0():
+            copies.extend(spread(0, "gy", lambda to: part.at[to], a))
+            a[me["gy"]] = part[me["gy"]]
+
+        def step1():
+            collect(0, "gy", a)
+            b[me["gx"]] = total(a)
+            copies.extend(spread(1, "gx", lambda to: b.at[me["gx"]], b))
+
+        def step2():
+            collect(1, "gx", b)
+            c[me["gz"]] = total(b)
+            copies.extend(spread(2, "gz", lambda to: c.at[me["gz"]], c))
+
+        def step3():
+            collect(2, "gz", c)
+            d[me["gy"]] = total(c)
+            copies.extend(spread(3, "gy", lambda to: d.at[me["gy"]], d))
+
+        def step4():
+            collect(3, "gy", d)
+            for copy in copies:
+                copy.wait_send()
+            return d[...].reshape(-1, T)[:, :NV] * (1.0 / dofs)
+
+        return step0, step1, step2, step3, step4
 
     def residual(n, coeffs):
         depth = 2 * NV * n
@@ -445,9 +458,13 @@
         lax.fori_loop(0, 2 * NC, body, 0)
         put(slice(Y_LO, HALO), QH[:, Y_LO:HALO])
 
+    mass = [reducer(n) for n in range(3)]
+    stiff = [reducer(n + 3) for n in range(3)]
     first[0]()
-    gram(0, True, P0)
+    gram(0, True, sums[0][0])
+    mass[0][0]()
     first[1]()
+    mass[0][1]()
     for i, at_x in enumerate((X_LO, X_HI)):
         for c in range(NC):
             QH[:, at_x + c * CH : at_x + (c + 1) * CH] = QX[i]
@@ -459,43 +476,59 @@
     stiffness(0, True)
     second, third = later(1), later(2)
     second[0]()
-    gram(0, False, P0)
-
-    def during_first():
-        second[1]()
-        first[2]()
-
-        def body(b, _):
-            for k in range(HALO // T):
-                HB[block(NV + b * 8), tile(k)] = QH[:, tile(k)] * HS[0, block(b * 8), tile(k)]
-            return 0
-
-        lax.fori_loop(0, NV // 8, body, 0)
-
-    G = all_reduce(0, P0, A0, B0, C0, D0, during_first)
-    li0 = factor_inverse(G[:, :NV])
-    theta0 = nt(mm(li0, G[:, NV:]), li0)
+    gram(0, False, sums[3][0])
+    mass[0][2]()
+    stiff[0][0]()
+    mass[0][3]()
+    stiff[0][1]()
+    stiff[0][2]()
+    second[1]()
+    first[2]()
+
+    def scale(b, _):
+        for k in range(HALO // T):
+            HB[block(NV + b * 8), tile(k)] = QH[:, tile(k)] * HS[0, block(b * 8), tile(k)]
+        return 0
+
+    lax.fori_loop(0, NV // 8, scale, 0)
+    gm = mass[0][4]()
+    stiff[0][3]()
+    SM[0] = factor_inverse(gm)
+    gk = stiff[0][4]()
+    li0 = SM[0]
+    theta0 = nt(mm(li0, gk), li0)
     c0 = parts_of(jnp.concatenate([li0, -mm(theta0, li0)], axis=1))
-    SM[0], SM[1] = li0, theta0
+    SM[1] = theta0
     residual(1, c0)
-    gram(1, True, P1)
+    gram(1, True, sums[1][0])
+    mass[1][0]()
     second[2]()
     HB[0:NV, Z_AT:HALO] = ZR[1, 0, 0:NV, :] + ZR[1, 1, 0:NV, :]
     residual_halo(1, c0)
+    mass[1][1]()
     stiffness(1, True)
     third[0]()
-    gram(1, False, P1)
-
-    G = all_reduce(1, P1, A1, B1, C1, D1, third[1])
+    gram(1, False, sums[4][0])
+
+    mass[1][2]()
+    stiff[1][0]()
+    mass[1][3]()
+    stiff[1][1]()
+    stiff[1][2]()
+    third[1]()
+    gm = mass[1][4]()
+    stiff[1][3]()
+    mxr = mm(SM[0], gm[:NV, :])
+    li_r = factor_inverse(gm[NV:, :] - tn(mxr, mxr))
+    SM[5], SM[10], SM[11] = mxr, li_r, -nt(li_r, mxr)
+    gk = stiff[1][4]()
     li0, theta0 = SM[0], SM[1]
-    cross = mm(li0, G[:NV, :])
-    mxr, kxr = cross[:, :NV], cross[:, NV:]
-    li_r = factor_inverse(G[NV:, :NV] - tn(mxr, mxr))
+    kxr = mm(li0, gk[:NV, :])
     li = jnp.concatenate(
-        [jnp.concatenate([one, zero], axis=1), jnp.concatenate([-nt(li_r, mxr), li_r], axis=1)], axis=0
+        [jnp.concatenate([one, zero], axis=1), jnp.concatenate([SM[11], SM[10]], axis=1)], axis=0
     )
     ga = jnp.concatenate(
-        [jnp.concatenate([theta0, kxr], axis=1), jnp.concatenate([kxr.T, G[NV:, NV:]], axis=1)], axis=0
+        [jnp.concatenate([theta0, kxr], axis=1), jnp.concatenate([kxr.T, gk[NV:, :]], axis=1)], axis=0
     )
     h = nt(mm(li, ga), li)
     qt, th, theta1 = filtered(h)
@@ -503,44 +536,55 @@
     a2t = ct[:, NV:]
     a1t = mm(ct[:, :NV], li0)
     c1 = parts_of(jnp.concatenate([a1t, -mm(theta1, a1t), a2t, -mm(theta1, a2t)], axis=1))
-    SM[2], SM[3], SM[4], SM[5] = theta1, a1t, a2t, mxr
+    SM[2], SM[3], SM[4] = theta1, a1t, a2t
     SQ[0], SQ[1], SH[...] = qt, th, h
     residual(2, c1)
-    gram(2, True, P2)
+    gram(2, True, sums[2][0])
+    mass[2][0]()
+    qt, th = SQ[0], SQ[1]
+    ut = jnp.concatenate([nt(SM[4], SM[5]), qt[:, NV:]], axis=1)
+    mxp, mpp = nt(qt, ut), nt(ut, ut)
+    SM[6], SM[7], SM[8], SM[9] = mxp, mpp - tn(mxp, mxp), nt(th, ut), nt(mm(ut, SH[...]), ut)
     third[2]()
     HB[2 * NV : 3 * NV, Z_AT:HALO] = ZR[2, 0, 0:NV, :] + ZR[2, 1, 0:NV, :]
     residual_halo(2, c1)
+    mass[2][1]()
     stiffness(2, False)
-    gram(2, False, P2)
-
-    def during_third():
-        qt, th = SQ[0], SQ[1]
-        ut = jnp.concatenate([nt(SM[4], SM[5]), qt[:, NV:]], axis=1)
-        mxp, mpp = nt(qt, ut), nt(ut, ut)
-        SM[6], SM[7], SM[8], SM[9] = mxp, mpp - tn(mxp, mxp), nt(th, ut), nt(mm(ut, SH[...]), ut)
-
-    G = all_reduce(2, P2, A2, B2, C2, D2, during_third)
-    theta1, a1t, a2t, _, mxp, spp, kxp, kpp = (SM[i] for i in range(2, 10))
-    cross_p = mm(a2t, G[NV : 2 * NV, :])
-    cross = mm(jnp.concatenate([a1t, a2t], axis=1), G[: 2 * NV, :])
-    mxr, kxr = cross[:, :NV], cross[:, NV:]
-    mpr, kpr = cross_p[:, :NV], cross_p[:, NV:]
-    li_r = factor_inverse(G[2 * NV :, :NV] - tn(mxr, mxr))
+    gram(2, False, sums[5][0])
+
+    mass[2][2]()
+    stiff[2][0]()
+    stiff[2][1]()
+    mass[2][3]()
+    stiff[2][2]()
+    gm = mass[2][4]()
+    stiff[2][3]()
+    both = jnp.concatenate([SM[3], SM[4]], axis=1)
+    mxr = mm(both, gm[: 2 * NV, :])
+    mpr = mm(SM[4], gm[NV : 2 * NV, :])
+    mxp = SM[6]
+    li_r = factor_inverse(gm[2 * NV :, :] - tn(mxr, mxr))
     l32 = nt(mpr - tn(mxp, mxr), li_r)
-    li_p = factor_inverse(spp - nt(l32, l32))
+    li_p = factor_inverse(SM[7] - nt(l32, l32))
     below = -nt(li_r, mxr)
+    SM[10], SM[11], SM[12] = li_r, below, li_p
+    SM[13], SM[14] = mm(li_p, -mxp.T - mm(l32, below)), -mm(li_p, mm(l32, li_r))
+    gk = stiff[2][4]()
+    theta1, a1t, a2t, kxp, kpp = SM[2], SM[3], SM[4], SM[8], SM[9]
+    kxr = mm(jnp.concatenate([a1t, a2t], axis=1), gk[: 2 * NV, :])
+    kpr = mm(a2t, gk[NV : 2 * NV, :])
     li = jnp.concatenate(
         [
             jnp.concatenate([one, zero, zero], axis=1),
-            jnp.concatenate([below, li_r, zero], axis=1),
-            jnp.concatenate([mm(li_p, -mxp.T - mm(l32, below)), -mm(li_p, mm(l32, li_r)), li_p], axis=1),
+            jnp.concatenate([SM[11], SM[10], zero], axis=1),
+            jnp.concatenate([SM[13], SM[14], SM[12]], axis=1),
         ],
         axis=0,
     )
     ga = jnp.concatenate(
         [
             jnp.concatenate([theta1, kxr, kxp], axis=1),
-            jnp.concatenate([kxr.T, G[2 * NV :, NV:], kpr.T], axis=1),
+            jnp.concatenate([kxr.T, gk[2 * NV :, :], kpr.T], axis=1),
             jnp.concatenate([kxp.T, kpr, kpp], axis=1),
         ],
         axis=0,
@@ -588,11 +632,11 @@
         pltpu.VMEM((3, 2, NV + 8, T), F32),
     ]
     heights = [NV * (i + 1) // 8 for i in range(3)]
-    for lead in (8, sizes["gy"], sizes["gx"], sizes["gz"], 8):
-        scratch += [pltpu.VMEM((lead, h, T), F32) for h in heights]
-    scratch += [pltpu.VMEM((10, NV, NV), F32)]
+    for height in 2 * heights:
+        scratch += [pltpu.VMEM((lead, height, T), F32) for lead in (8, sizes["gy"], sizes["gx"], sizes["gz"], 8)]
+    scratch += [pltpu.VMEM((15, NV, NV), F32)]
     scratch += [pltpu.VMEM((2, NV, 2 * NV), F32), pltpu.VMEM((2 * NV, 2 * NV), F32)]
-    scratch += [pltpu.SemaphoreType.DMA((3, 2, 4, 8)), pltpu.SemaphoreType.DMA((7, 2, 8))]
+    scratch += [pltpu.SemaphoreType.DMA((6, 2, 4, 8)), pltpu.SemaphoreType.DMA((7, 2, 8))]
     vmem = pl.BlockSpec(memory_space=pltpu.VMEM)
     modes, ritz = pl.pallas_call(
         functools.partial(kernel, dofs, sizes),

time: 135 us -> 132 us (0.978)
  Pallas kernels: 131 us -> 128 us
    pallas_call x1, Pallas kernels: 131 us -> 128 us  [local(): pl.pallas_call(functools.partial(kernel, dofs, sizes), out_shape=(jax.Sha...]
where the time goes in v2:
time: 132 us
  Pallas kernels  128 us (97%)
  local copies, waits for them, and re-layouts  3.28 us (2%)
    pallas_call x1, Pallas kernels, local(): pl.pallas_call(functools.partial(kernel, dofs, sizes), out_shape=(jax.Sha...  128 us
    unnamed x4, local copies, waits for them, and re-layouts  3.28 us

profile of v2, /device:TPU:1, one launch (start us, length us, event | category | flops | bytes accessed | tf_op | source)
XLA Modules:
  0.0 131.7 jit_solution(8747097527320471963)
XLA Ops:
  0.6 127.8 %lobpcg.1 = (f32[3072,128]{1,0:T(8,128)}, f32[64,64]{1,0:T(8,128)}) custom-call(f32[3072,128]{1,0:T(8,128)} %bitcast.5, f32[16,128]{1,0:T(8,128)} %bitcast.7, f32[16,128]{1,0:T(8,128)} %bitcast.8, f32[16,128]{1,0:T(8,128)} %bitcast.9), custom_call_target="tpu_custom_call" | custom-call | tf_op jit(solution)/shard_map/lobpcg/pallas_call | solution.py:641
  128.4 0.0 copy-start
  128.5 2.7 %copy.8 = f32[64,3,2,8,128]{4,3,2,1,0:T(8,128)} copy(f32[64,3,2,8,128]{4,3,2,1,0:T(8,128)} %bitcast.6) | data formatting | bytes 3145728
  131.1 0.0 copy-done
  131.1 0.6 copy.9
Async XLA Ops:
  128.4 2.7 %copy-start = (f32[64,64]{1,0:T(8,128)S(1)}, f32[64,64]{1,0:T(8,128)}, u32[]{:S(2)}) copy-start(f32[64,64]{1,0:T(8,128)} %get-tuple-element.9) | copy-start | bytes 49156
